TPU v7x, 256 devices: a whole 4x4x8 slice. The times are simulated.
256 devices in a mesh: rows: 256 (over x, y, z, core).
Axes of the slice: x: 4, y: 4, z: 8, core: 2. Of those that a mesh axis runs over, the one named last changes fastest.
Arguments:
- q_final: float32 [393216, 512], P('rows'), may hold values from -0.050370466 to 0.050370466
- r_first: float32 [512, 512], replicated, may hold values from -1 to 2, as said below
- r_second: float32 [512, 512], replicated, may hold values from -1 to 2, as said below
- q_grad: float32 [393216, 512], P('rows'), may hold values from -6 to 6
- r_grad: float32 [512, 512], replicated, may hold values from -1.5 to 1.5
Outputs:
- a_grad: float32 [393216, 512], P('rows')
Inputs may be any that keep to these rules, and one draw needn't show every extreme that they name: `r_first`: upper triangular, diagonal between 1 and 2. `r_second`: upper triangular, diagonal between 1 and 2.
All inputs are finite; a program needn't handle non-finite values.
Results may differ from a plain program's by a relative error of at most 0.000084.
Values sent between devices are 32-bit elements; how exact they have to be, the bound alone decides.
A program may use at most 128 MiB of HBM per device.

v0:
```python
import jax
import jax.numpy as jnp
from jax import lax
from jax.experimental import pallas as pl
from jax.experimental.pallas import tpu as pltpu
from jax.sharding import PartitionSpec as P

HIGHEST = lax.Precision.HIGHEST
W, HALF = 512, 256
NX, NY, NZ = 4, 4, 8
ROWS, STEPS = 1536, 3
PARTS = ((0, 5, True), (5, 4, False))
NN, NT, TN = ((1,), (0,)), ((1,), (1,)), ((0,), (0,))
A, B = slice(0, HALF), slice(HALF, W)


def mm(a, b):
    return lax.dot_general(a, b, (NN, ((), ())), precision=HIGHEST, preferred_element_type=jnp.float32)


def halves(a):
    high = a.astype(jnp.bfloat16)
    return high, (a - high.astype(jnp.float32)).astype(jnp.bfloat16)


def cut(pair, *index):
    return pair[0][index], pair[1][index]


def join(pairs, axis):
    return tuple(jnp.concatenate([p[i] for p in pairs], axis=axis) for i in range(2))


def mm3(a, b, dims=NN):
    (ah, al), (bh, bl) = a, b

    def dot(u, v):
        return lax.dot_general(u, v, (dims, ((), ())), preferred_element_type=jnp.float32)

    return dot(ah, bh) + (dot(ah, bl) + dot(al, bh))


def iotas(rows, cols):
    return lax.broadcasted_iota(jnp.int32, (rows, cols), 0), lax.broadcasted_iota(jnp.int32, (rows, cols), 1)


def small_inverses(uppers, size=128):
    row, col = iotas(size, size)
    eye, above = row == col, col > row
    block = [u[b : b + size, b : b + size] for u in uppers for b in range(0, W, size)]
    inv = []
    for u in block:
        d_row = 1.0 / jnp.sum(jnp.where(eye, u, 0.0), axis=0, keepdims=True)
        d_col = 1.0 / jnp.sum(jnp.where(eye, u, 0.0), axis=1, keepdims=True)
        pair = above & (row // 2 == col // 2)
        inv.append(jnp.where(eye, d_row, jnp.where(pair, -(u * d_col) * d_row, 0.0)))
    s = 2
    while s < size:
        between = above & (row // (2 * s) == col // (2 * s)) & (row // s != col // s)
        half = [mm(jnp.where(between, u, 0.0), x) for u, x in zip(block, inv)]
        inv = [x - mm(x, h) for x, h in zip(inv, half)]
        s *= 2
    return inv


def join_inverses(uppers, outs, size=128):
    s = size
    while s < W:
        for u, out in zip(uppers, outs):
            for b in range(0, W, 2 * s):
                top, low = slice(b, b + s), slice(b + s, b + 2 * s)
                out[top, low] = -mm(out[top, top], mm(u[top, low], out[low, low]))
        s *= 2


def place():
    me = lax.axis_index("rows")
    c = lax.rem(me, 2)
    z = lax.rem(lax.div(me, 2), NZ)
    y = lax.rem(lax.div(me, 2 * NZ), NY)
    x = lax.div(me, 2 * NZ * NY)
    return x, y, z, c


def device(x, y, z, c):
    return (((x * NY + y) * NZ + z) * 2 + c,)


def pack_half(h, wide, square, put):
    row, col = iotas(HALF, HALF)
    low, eye = row >= col, row == col
    is_top = jnp.full((HALF, HALF), h, jnp.int32) == 0
    parts = (jnp.where(low & is_top, square, wide[:, A]), jnp.where(low | is_top, wide[:, B], square))
    diag = jnp.sum(jnp.where(eye, jnp.where(is_top, wide[:, A], square), 0.0), axis=0, keepdims=True)
    first = lax.broadcasted_iota(jnp.int32, (8, 128), 0) == 0
    for group in range(16):
        for tile in range(8):
            r, l = group * 16 + (tile // 4) * 8, (tile % 4) * 128
            put(group // 4, group % 4, tile, parts[l // HALF][r : r + 8, l % HALF : l % HALF + 128])
        extra = jnp.zeros((8, 128), jnp.float32)
        if group < 2:
            extra = jnp.where(first, jnp.broadcast_to(diag[:, group * 128 : group * 128 + 128], (8, 128)), 0.0)
        put(group // 4, group % 4, 8, extra)


def copy_lower(m, low, strict):
    return jnp.where(low, m, 0.0) + jnp.where(strict, m, 0.0).T


def symmetric(b00, b10, b11):
    row, col = iotas(HALF, HALF)
    low, strict = row >= col, row > col
    top = jnp.concatenate([copy_lower(b00, low, strict), b10.T], axis=1)
    return jnp.concatenate([top, jnp.concatenate([b10, copy_lower(b11, low, strict)], axis=1)], axis=0)


def middle(square, diag, k1, k2, r2, inv1, inv2, both):
    row, col = iotas(HALF, HALF)
    low, strict, above, eye = row >= col, row > col, row < col, row == col
    second = halves(symmetric(*(k2[i, j] - square[i, j] for i, j in ((A, A), (B, A), (B, B)))))
    grams = []
    for s in (A, B):
        upper = jnp.where(above, square[s, s], 0.0)
        grams.append(upper + upper.T + jnp.where(eye, jnp.broadcast_to(diag[:, s], (HALF, HALF)), 0.0))
    g01 = square[A, B]
    gram_a = halves(jnp.concatenate([grams[0], g01.T], axis=0))
    gram_b = halves(jnp.concatenate([g01, grams[1]], axis=0))
    cross_a = jnp.concatenate([jnp.where(low, square[A, A], 0.0), square[B, A]], axis=0)
    y_a = halves(cross_a + mm3(second, gram_a))
    y_bb = halves(jnp.where(low, square[B, B], 0.0) + mm3(cut(second, B), gram_b))
    w_a = halves(mm3(y_a, cut(r2, A, A)))
    w_bb = halves(mm3(join([cut(y_a, B), y_bb], 1), cut(r2, slice(None), B)))
    z_aa = mm3(cut(inv2, A), w_a)
    z_b = mm3(cut(inv2, B, B), join([cut(w_a, B), w_bb], 1))
    first = halves(symmetric(k1[A, A] - z_aa, k1[B, A] - z_b[:, A], k1[B, B] - z_b[:, B]))
    v = halves(times_lower(first, inv1))
    add = times_lower(second, both)
    return add[A] + mm3(cut(r2, A), v), add[B] + mm3(cut(r2, B, B), cut(v, B))


def times_lower(a, upper):
    return jnp.concatenate([mm3(a, cut(upper, A), NT), mm3(cut(a, slice(None), B), cut(upper, B, B), NT)], axis=1)


def main_kernel(q_hbm, r1_hbm, r2_hbm, g_hbm, rg_hbm, m2_out, u_hbm, *scratch):
    scratch = list(scratch)
    q_in, g_in, slab_h, slab_l, r1, r2, rg, inv1, inv2, k1, k2, u_buf, square, diag, acc = (scratch.pop(0) for _ in range(15))
    bf = [scratch.pop(0) for _ in range(8)]
    r2_p, inv1_p, inv2_p, both_p = (tuple(bf[i : i + 2]) for i in range(0, 8, 2))
    theirs, core_in, mine, own, z_in, whole = (scratch.pop(0) for _ in range(6))
    one_in, two, two_in = ([scratch.pop(0) for _ in PARTS] for _ in range(3))
    in_sem, u_sem, core_sem, one_sem, two_sem, z_sem, four_sem, five_sem, last_sem = (scratch.pop(0) for _ in range(9))
    x, y, z, c = place()
    other = device(x, y, z, 1 - c)
    xs = [lax.rem(x + k, NX) for k in range(1, NX)]
    ys = [lax.rem(y + k, NY) for k in range(1, NY)]
    to_x = [device(p, y, z, c) for p in xs]
    to_y = [device(x, p, z, c) for p in ys]
    to_z = [device(x, y, lax.rem(z + k, NZ), c) for k in range(1, NZ)]

    rows = ROWS // STEPS
    loads = []
    for step in range(STEPS):
        at = pl.ds(step * rows, rows)
        for i, (src, dst) in enumerate(((q_hbm, q_in), (g_hbm, g_in))):
            loads.append(pltpu.make_async_copy(src.at[at], dst.at[at], in_sem.at[2 * step + i]))
    for i, (src, dst) in enumerate(((r1_hbm, r1), (r2_hbm, r2), (rg_hbm, rg))):
        loads.append(pltpu.make_async_copy(src, dst, in_sem.at[2 * STEPS + i]))
    for load in loads:
        load.start()

    barrier = pltpu.get_barrier_semaphore()
    peers = [other, *to_x, *to_y, *to_z]
    for peer in peers:
        pl.semaphore_signal(barrier, inc=1, device_id=peer, device_id_type=pl.DeviceIdType.MESH)

    sent = []

    def send(src, dst, sems, k, to):
        copy = pltpu.make_async_remote_copy(src_ref=src, dst_ref=dst, send_sem=sems.at[0, k], recv_sem=sems.at[1, k],
                                            device_id=to, device_id_type=pl.DeviceIdType.MESH)
        copy.start()
        sent.append(copy)
        return copy

    def gram_half(h, at):
        def slab(i):
            return slab_h[i, at], slab_l[i, at]

        q = join([slab(0), slab(3)], 1)
        return mm3(slab(h), q, TN), mm3(slab(2 + h), slab(3 * h), TN)

    for step in range(STEPS):
        at = slice(step * rows, (step + 1) * rows)
        loads[2 * step].wait()
        loads[2 * step + 1].wait()
        for i, (src, s) in enumerate(((q_in, A), (g_in, B), (g_in, A), (q_in, B))):
            slab_h[i, at], slab_l[i, at] = halves(src[at, s])
        wide, block = gram_half(1 - c, at)
        if step:
            wide, block = acc[:, :W] + wide, acc[:, W:] + block
        if step < STEPS - 1:
            acc[:, :W], acc[:, W:] = wide, block

    def put_theirs(i, j, tile, value):
        theirs[i, j, tile] = value

    pack_half(1 - c, wide, block, put_theirs)
    pl.semaphore_wait(barrier, len(peers))
    core = send(theirs, core_in, core_sem, 0, other)
    wide, block = gram_half(c, slice(None))
    core.wait_recv()

    def put_mine(i, j, tile, value):
        mine[i, j, tile] = value + core_in[i, j, tile]

    pack_half(c, wide, block, put_mine)

    def span(part):
        return pl.ds(part[0], part[1])

    def line(ref, part, at):
        return ref.at[at, :, span(part)] if part[2] else ref.at[:, at, span(part)]

    one = [[send(line(mine, part, (xs if part[2] else ys)[k]), one_in[p].at[k], one_sem, 3 * p + k, (to_x if part[2] else to_y)[k])
            for k in range(3)] for p, part in enumerate(PARTS)]

    for load in loads[2 * STEPS :]:
        load.wait()
    small = small_inverses((r1[...], r2[...]))
    for m, out in enumerate((inv1, inv2)):
        out[...] = jnp.zeros((W, W), jnp.float32)
        for b in range(4):
            out[b * 128 : b * 128 + 128, b * 128 : b * 128 + 128] = small[4 * m + b]

    two_copies = []
    for p, part in enumerate(PARTS):
        lo, hi = part[0], part[0] + part[1]
        for copy in one[p]:
            copy.wait_recv()
        here = mine[x, :, lo:hi] if part[2] else mine[:, y, lo:hi]
        two[p][...] = (here + one_in[p][0]) + (one_in[p][1] + one_in[p][2])
        two_copies.append([send(two[p].at[(ys if part[2] else xs)[k]], two_in[p].at[k], two_sem, 3 * p + k, (to_y if part[2] else to_x)[k])
                           for k in range(3)])

    join_inverses((r1, r2), (inv1, inv2))
    for pair, ref in ((inv1_p, inv1), (inv2_p, inv2), (r2_p, r2)):
        pair[0][...], pair[1][...] = halves(ref[...])

    z_copies = []
    for p, part in enumerate(PARTS):
        lo, hi = part[0], part[0] + part[1]
        for copy in two_copies[p]:
            copy.wait_recv()
        own[lo:hi] = (two[p][y if part[2] else x] + two_in[p][0]) + (two_in[p][1] + two_in[p][2])
        z_copies.append([send(own.at[span(part)], z_in.at[k, span(part)], z_sem, 7 * p + k, to_z[k]) for k in range(NZ - 1)])

    def pair_of(refs):
        return refs[0][...], refs[1][...]

    both = halves(mm3(pair_of(inv1_p), pair_of(inv2_p)))
    both_p[0][...], both_p[1][...] = both
    for step in range(STEPS):
        at = slice(step * rows, (step + 1) * rows)
        g0, g1 = (slab_h[2, at], slab_l[2, at]), (slab_h[1, at], slab_l[1, at])
        u_buf[at, A] = mm3(join([g0, g1], 1), cut(both, A), NT)
        u_buf[at, B] = mm3(g1, cut(both, B, B), NT)
    u_copy = pltpu.make_async_copy(u_buf, u_hbm, u_sem)
    u_copy.start()
    r2_v = pair_of(r2_p)
    t = halves(mm3(halves(r1[...]), halves(rg[...]), NT))
    k2[...] = mm3(r2_v, t)
    k1[...] = mm3(t, r2_v)

    four = []
    for p, part in enumerate(PARTS):
        lo, hi = part[0], part[0] + part[1]
        total = own[lo:hi]
        for k, copy in enumerate(z_copies[p]):
            copy.wait_recv()
            total = total + z_in[k, lo:hi]
        whole[c, x, y, lo:hi] = total
        ref = whole.at[c, x, y, span(part)]
        four.append([send(ref, ref, four_sem, 3 * p + k, (to_y if part[2] else to_x)[k]) for k in range(3)])
    five = []
    last = []
    mine_all = whole.at[c]
    for p, part in enumerate(PARTS):
        for copy in four[p]:
            copy.wait_recv()
        ref = line(mine_all, part, x if part[2] else y)
        five.append([send(ref, ref, five_sem, 3 * p + k, (to_x if part[2] else to_y)[k]) for k in range(3)])
        last.append(send(ref, ref, last_sem, 4 * p, other))
    for k in (0, 2, 1):
        for p, part in enumerate(PARTS):
            five[p][k].wait_recv()
            ref = line(mine_all, part, lax.rem((x if part[2] else y) + 3 - k, 4))
            last.append(send(ref, ref, last_sem, 4 * p + 1 + k, other))
    for copy in last:
        copy.wait_recv()

    for group in range(32):
        at = (group // 16, (group // 4) % 4, group % 4)
        for tile in range(8):
            r, l = group * 16 + (tile // 4) * 8, (tile % 4) * 128
            square[r : r + 8, l : l + 128] = whole[(*at, tile)]
        if group % 16 < 2:
            l = group // 16 * HALF + group % 16 * 128
            diag[:, l : l + 128] = whole[(*at, 8)]
    m2_out[A], m2_out[B] = middle(square, diag[0:1], k1, k2, pair_of(r2_p), pair_of(inv1_p), pair_of(inv2_p), pair_of(both_p))
    u_copy.wait()
    for copy in sent:
        copy.wait_send()


def main(q_final, r_first, r_second, q_grad, r_grad):
    hbm = pl.BlockSpec(memory_space=pl.ANY)
    f32, bf16 = jnp.float32, jnp.bfloat16
    tile = (8, 128)
    scratch = [pltpu.VMEM((ROWS, W), f32)] * 2
    scratch += [pltpu.VMEM((4, ROWS, HALF), bf16)] * 2
    scratch += [pltpu.VMEM((W, W), f32)] * 7
    scratch += [pltpu.VMEM((ROWS, W), f32), pltpu.VMEM((W, W), f32), pltpu.VMEM((8, W), f32), pltpu.VMEM((HALF, W + HALF), f32)]
    scratch += [pltpu.VMEM((W, W), bf16)] * 8
    scratch += [pltpu.VMEM((NX, NY, 9, *tile), f32)] * 3
    scratch += [pltpu.VMEM((9, *tile), f32), pltpu.VMEM((NZ - 1, 9, *tile), f32), pltpu.VMEM((2, NX, NY, 9, *tile), f32)]
    scratch += [pltpu.VMEM((3, 4, part[1], *tile), f32) for part in PARTS]
    scratch += [pltpu.VMEM((4, part[1], *tile), f32) for part in PARTS]
    scratch += [pltpu.VMEM((3, part[1], *tile), f32) for part in PARTS]
    n = len(PARTS)
    scratch += [pltpu.SemaphoreType.DMA((2 * STEPS + 3,)), pltpu.SemaphoreType.DMA]
    scratch += [pltpu.SemaphoreType.DMA((2, k)) for k in (1, 3 * n, 3 * n, 7 * n, 3 * n, 3 * n, 4 * n)]
    return pl.pallas_call(
        main_kernel,
        in_specs=[hbm] * 5,
        out_specs=[pl.BlockSpec(memory_space=pltpu.VMEM), hbm],
        out_shape=[jax.ShapeDtypeStruct((W, W), f32), jax.ShapeDtypeStruct((ROWS, W), f32)],
        scratch_shapes=scratch,
        compiler_params=pltpu.CompilerParams(collective_id=0, has_side_effects=True, vmem_limit_bytes=60 << 20),
        name="main",
    )(q_final, r_first, r_second, q_grad, r_grad)


def finish_kernel(u, q, m2, out):
    out[...] = u[...] + mm3(halves(q[...]), halves(m2[...]))


def finish(u, q_final, m2):
    rows = ROWS // 6
    spec = pl.BlockSpec((rows, W), lambda i: (i, 0))
    small = pl.BlockSpec((W, W), lambda i: (0, 0))
    return pl.pallas_call(
        finish_kernel,
        grid=(6,),
        in_specs=[spec, spec, small],
        out_specs=spec,
        out_shape=jax.ShapeDtypeStruct((ROWS, W), jnp.float32),
        compiler_params=pltpu.CompilerParams(vmem_limit_bytes=48 << 20),
        name="finish",
    )(u, q_final, m2)


def local(q_final, r_first, r_second, q_grad, r_grad):
    m2, u = main(q_final, r_first, r_second, q_grad, r_grad)
    return finish(u, q_final, m2)


def solution(mesh):
    placed = (P("rows", None), P(), P(), P("rows", None), P())
    return jax.shard_map(local, mesh=mesh, in_specs=placed, out_specs=P("rows", None), check_vma=False)
```

profile of v0, /device:TPU:1, one launch (start us, length us, event | category | flops | bytes accessed | tf_op | source)
XLA Modules:
  0.0 59.9 jit_solution(5189101907510881829)
XLA Ops:
  0.0 50.0 %main.1 = (f32[512,512]{1,0:T(8,128)}, f32[1536,512]{1,0:T(8,128)}) custom-call(f32[1536,512]{1,0:T(8,128)} %q.1, f32[512,512]{1,0:T(8,128)} %r1_hbm.1, f32[512,512]{1,0:T(8,128)} %r2_hbm.1, f32[1536,512]{1,0:T(8,128)} %g_hbm.1, f32[512,512]{1,0:T(8,128)} %rg_hbm.1), custom_call_target="tpu_custom_call" | custom-call | tf_op jit(solution)/shard_map/main/pallas_call | solution.py:333
  50.0 0.0 copy-start
  50.0 1.9 %copy-done = f32[1536,512]{1,0:T(8,128)S(1)} copy-done((f32[1536,512]{1,0:T(8,128)S(1)}, f32[1536,512]{1,0:T(8,128)}, u32[]{:S(2)}) %copy-start) | copy-done | bytes 3145752
  51.9 0.0 copy-start.1
  51.9 1.2 %copy-done.1 = f32[512,512]{1,0:T(8,128)S(1)} copy-done((f32[512,512]{1,0:T(8,128)S(1)}, f32[512,512]{1,0:T(8,128)}, u32[]{:S(2)}) %copy-start.1) | copy-done | bytes 1048600
  53.1 6.8 %finish.1 = f32[1536,512]{1,0:T(8,128)} custom-call(f32[1536,512]{1,0:T(8,128)S(1)} %copy-done, f32[1536,512]{1,0:T(8,128)} %q.1, f32[512,512]{1,0:T(8,128)S(1)} %copy-done.1), custom_call_target="tpu_custom_call" | custom-call | tf_op jit(solution)/shard_map/finish/pallas_call | solution.py:352
Async XLA Ops:
  50.0 1.9 %copy-start = (f32[1536,512]{1,0:T(8,128)S(1)}, f32[1536,512]{1,0:T(8,128)}, u32[]{:S(2)}) copy-start(f32[1536,512]{1,0:T(8,128)} %get-tuple-element.7.u) | copy-start | bytes 9437188
  51.9 1.2 %copy-start.1 = (f32[512,512]{1,0:T(8,128)S(1)}, f32[512,512]{1,0:T(8,128)}, u32[]{:S(2)}) copy-start(f32[512,512]{1,0:T(8,128)} %get-tuple-element.8.m2) | copy-start | bytes 3145732
where the time goes:
time: 60.2 us; the launch traced here: 59.9 us
  Pallas kernels  56.8 us (94%)
  local copies, waits for them, and re-layouts  3.11 us (5%)
    pallas_call x1, Pallas kernels, main(): pl.pallas_call(main_kernel, in_specs=[hbm] * 5, out_specs=[pl.BlockSpec(m...  50 us
    pallas_call x1, Pallas kernels, finish(): pl.pallas_call(finish_kernel, grid=(6,), in_specs=[spec, spec, small], ou...  6.76 us
    unnamed x4, local copies, waits for them, and re-layouts  3.11 us

commit v1 on v0

--- a/solution.py
+++ b/solution.py
@@ -10,6 +10,7 @@
 NX, NY, NZ = 4, 4, 8
 ROWS, STEPS = 1536, 3
 PARTS = ((0, 5, True), (5, 4, False))
+FAR_4, FAR_8 = (1, 0, 2), (3, 2, 4, 1, 5, 0, 6)
 NN, NT, TN = ((1,), (0,)), ((1,), (1,)), ((0,), (0,))
 A, B = slice(0, HALF), slice(HALF, W)
 
@@ -142,14 +143,14 @@
     return jnp.concatenate([mm3(a, cut(upper, A), NT), mm3(cut(a, slice(None), B), cut(upper, B, B), NT)], axis=1)
 
 
-def main_kernel(q_hbm, r1_hbm, r2_hbm, g_hbm, rg_hbm, m2_out, u_hbm, *scratch):
+def main_kernel(q_hbm, r1_hbm, r2_hbm, g_hbm, rg_hbm, u_buf, slab_h, slab_l, m2_h, m2_l, *scratch):
     scratch = list(scratch)
-    q_in, g_in, slab_h, slab_l, r1, r2, rg, inv1, inv2, k1, k2, u_buf, square, diag, acc = (scratch.pop(0) for _ in range(15))
+    q_in, g_in, r1, r2, rg, inv1, inv2, k1, k2, square, diag, acc = (scratch.pop(0) for _ in range(12))
     bf = [scratch.pop(0) for _ in range(8)]
     r2_p, inv1_p, inv2_p, both_p = (tuple(bf[i : i + 2]) for i in range(0, 8, 2))
     theirs, core_in, mine, own, z_in, whole = (scratch.pop(0) for _ in range(6))
     one_in, two, two_in = ([scratch.pop(0) for _ in PARTS] for _ in range(3))
-    in_sem, u_sem, core_sem, one_sem, two_sem, z_sem, four_sem, five_sem, last_sem = (scratch.pop(0) for _ in range(9))
+    in_sem, core_sem, one_sem, two_sem, z_sem, four_sem, five_sem, last_sem = (scratch.pop(0) for _ in range(8))
     x, y, z, c = place()
     other = device(x, y, z, 1 - c)
     xs = [lax.rem(x + k, NX) for k in range(1, NX)]
@@ -173,6 +174,9 @@
     peers = [other, *to_x, *to_y, *to_z]
     for peer in peers:
         pl.semaphore_signal(barrier, inc=1, device_id=peer, device_id_type=pl.DeviceIdType.MESH)
+
+    def pair_of(refs):
+        return refs[0][...], refs[1][...]
 
     sent = []
 
@@ -223,15 +227,11 @@
         return ref.at[at, :, span(part)] if part[2] else ref.at[:, at, span(part)]
 
     one = [[send(line(mine, part, (xs if part[2] else ys)[k]), one_in[p].at[k], one_sem, 3 * p + k, (to_x if part[2] else to_y)[k])
-            for k in range(3)] for p, part in enumerate(PARTS)]
+            for k in FAR_4] for p, part in enumerate(PARTS)]
 
     for load in loads[2 * STEPS :]:
         load.wait()
-    small = small_inverses((r1[...], r2[...]))
-    for m, out in enumerate((inv1, inv2)):
-        out[...] = jnp.zeros((W, W), jnp.float32)
-        for b in range(4):
-            out[b * 128 : b * 128 + 128, b * 128 : b * 128 + 128] = small[4 * m + b]
+    r2_p[0][...], r2_p[1][...] = halves(r2[...])
 
     two_copies = []
     for p, part in enumerate(PARTS):
@@ -241,11 +241,13 @@
         here = mine[x, :, lo:hi] if part[2] else mine[:, y, lo:hi]
         two[p][...] = (here + one_in[p][0]) + (one_in[p][1] + one_in[p][2])
         two_copies.append([send(two[p].at[(ys if part[2] else xs)[k]], two_in[p].at[k], two_sem, 3 * p + k, (to_y if part[2] else to_x)[k])
-                           for k in range(3)])
-
-    join_inverses((r1, r2), (inv1, inv2))
-    for pair, ref in ((inv1_p, inv1), (inv2_p, inv2), (r2_p, r2)):
-        pair[0][...], pair[1][...] = halves(ref[...])
+                           for k in FAR_4])
+
+    r2_v = pair_of(r2_p)
+    r1_v, rg_v = halves(r1[...]), halves(rg[...])
+    t = halves(jnp.concatenate([mm3(cut(r1_v, A), rg_v, NT), mm3(cut(r1_v, B, B), cut(rg_v, slice(None), B), NT)], axis=0))
+    k2[A, A], k2[B] = mm3(cut(r2_v, A), cut(t, slice(None), A)), mm3(cut(r2_v, B, B), cut(t, B))
+    k1[:, A], k1[B, B] = mm3(cut(t, slice(None), A), cut(r2_v, A, A)), mm3(cut(t, B), cut(r2_v, slice(None), B))
 
     z_copies = []
     for p, part in enumerate(PARTS):
@@ -253,35 +255,42 @@
         for copy in two_copies[p]:
             copy.wait_recv()
         own[lo:hi] = (two[p][y if part[2] else x] + two_in[p][0]) + (two_in[p][1] + two_in[p][2])
-        z_copies.append([send(own.at[span(part)], z_in.at[k, span(part)], z_sem, 7 * p + k, to_z[k]) for k in range(NZ - 1)])
-
-    def pair_of(refs):
-        return refs[0][...], refs[1][...]
-
-    both = halves(mm3(pair_of(inv1_p), pair_of(inv2_p)))
-    both_p[0][...], both_p[1][...] = both
+        z_copies.append([send(own.at[span(part)], z_in.at[k, span(part)], z_sem, 7 * p + k, to_z[k]) for k in FAR_8])
+
+    small = small_inverses((r1[...], r2[...]))
+    for m, out in enumerate((inv1, inv2)):
+        out[...] = jnp.zeros((W, W), jnp.float32)
+        for b in range(4):
+            out[b * 128 : b * 128 + 128, b * 128 : b * 128 + 128] = small[4 * m + b]
+
+    join_inverses((r1, r2), (inv1, inv2))
+    for pair, ref in ((inv1_p, inv1), (inv2_p, inv2)):
+        pair[0][...], pair[1][...] = halves(ref[...])
+
+    i1, i2 = pair_of(inv1_p), pair_of(inv2_p)
+    for i, j in ((A, A), (A, B), (B, B)):
+        inner = slice(i.start, j.stop)
+        both_p[0][i, j], both_p[1][i, j] = halves(mm3(cut(i1, i, inner), cut(i2, inner, j)))
+    both_p[0][B, A], both_p[1][B, A] = jnp.zeros((HALF, HALF), jnp.bfloat16), jnp.zeros((HALF, HALF), jnp.bfloat16)
+    both = pair_of(both_p)
+
+    four = []
+    for p, part in enumerate(PARTS):
+        lo, hi = part[0], part[0] + part[1]
+        for copy in z_copies[p]:
+            copy.wait_recv()
+        total = own[lo:hi]
+        for k in range(NZ - 1):
+            total = total + z_in[k, lo:hi]
+        whole[c, x, y, lo:hi] = total
+        ref = whole.at[c, x, y, span(part)]
+        four.append([send(ref, ref, four_sem, 3 * p + k, (to_y if part[2] else to_x)[k]) for k in FAR_4])
     for step in range(STEPS):
         at = slice(step * rows, (step + 1) * rows)
         g0, g1 = (slab_h[2, at], slab_l[2, at]), (slab_h[1, at], slab_l[1, at])
         u_buf[at, A] = mm3(join([g0, g1], 1), cut(both, A), NT)
         u_buf[at, B] = mm3(g1, cut(both, B, B), NT)
-    u_copy = pltpu.make_async_copy(u_buf, u_hbm, u_sem)
-    u_copy.start()
-    r2_v = pair_of(r2_p)
-    t = halves(mm3(halves(r1[...]), halves(rg[...]), NT))
-    k2[...] = mm3(r2_v, t)
-    k1[...] = mm3(t, r2_v)
-
-    four = []
-    for p, part in enumerate(PARTS):
-        lo, hi = part[0], part[0] + part[1]
-        total = own[lo:hi]
-        for k, copy in enumerate(z_copies[p]):
-            copy.wait_recv()
-            total = total + z_in[k, lo:hi]
-        whole[c, x, y, lo:hi] = total
-        ref = whole.at[c, x, y, span(part)]
-        four.append([send(ref, ref, four_sem, 3 * p + k, (to_y if part[2] else to_x)[k]) for k in range(3)])
+
     five = []
     last = []
     mine_all = whole.at[c]
@@ -289,11 +298,11 @@
         for copy in four[p]:
             copy.wait_recv()
         ref = line(mine_all, part, x if part[2] else y)
-        five.append([send(ref, ref, five_sem, 3 * p + k, (to_x if part[2] else to_y)[k]) for k in range(3)])
+        five.append([send(ref, ref, five_sem, 3 * p + k, (to_x if part[2] else to_y)[k]) for k in FAR_4])
         last.append(send(ref, ref, last_sem, 4 * p, other))
     for k in (0, 2, 1):
         for p, part in enumerate(PARTS):
-            five[p][k].wait_recv()
+            five[p][FAR_4.index(k)].wait_recv()
             ref = line(mine_all, part, lax.rem((x if part[2] else y) + 3 - k, 4))
             last.append(send(ref, ref, last_sem, 4 * p + 1 + k, other))
     for copy in last:
@@ -307,8 +316,8 @@
         if group % 16 < 2:
             l = group // 16 * HALF + group % 16 * 128
             diag[:, l : l + 128] = whole[(*at, 8)]
-    m2_out[A], m2_out[B] = middle(square, diag[0:1], k1, k2, pair_of(r2_p), pair_of(inv1_p), pair_of(inv2_p), pair_of(both_p))
-    u_copy.wait()
+    for s, m in zip((A, B), middle(square, diag[0:1], k1, k2, pair_of(r2_p), pair_of(inv1_p), pair_of(inv2_p), pair_of(both_p))):
+        m2_h[s], m2_l[s] = halves(m)
     for copy in sent:
         copy.wait_send()
 
@@ -318,9 +327,8 @@
     f32, bf16 = jnp.float32, jnp.bfloat16
     tile = (8, 128)
     scratch = [pltpu.VMEM((ROWS, W), f32)] * 2
-    scratch += [pltpu.VMEM((4, ROWS, HALF), bf16)] * 2
     scratch += [pltpu.VMEM((W, W), f32)] * 7
-    scratch += [pltpu.VMEM((ROWS, W), f32), pltpu.VMEM((W, W), f32), pltpu.VMEM((8, W), f32), pltpu.VMEM((HALF, W + HALF), f32)]
+    scratch += [pltpu.VMEM((W, W), f32), pltpu.VMEM((8, W), f32), pltpu.VMEM((HALF, W + HALF), f32)]
     scratch += [pltpu.VMEM((W, W), bf16)] * 8
     scratch += [pltpu.VMEM((NX, NY, 9, *tile), f32)] * 3
     scratch += [pltpu.VMEM((9, *tile), f32), pltpu.VMEM((NZ - 1, 9, *tile), f32), pltpu.VMEM((2, NX, NY, 9, *tile), f32)]
@@ -328,41 +336,46 @@
     scratch += [pltpu.VMEM((4, part[1], *tile), f32) for part in PARTS]
     scratch += [pltpu.VMEM((3, part[1], *tile), f32) for part in PARTS]
     n = len(PARTS)
-    scratch += [pltpu.SemaphoreType.DMA((2 * STEPS + 3,)), pltpu.SemaphoreType.DMA]
+    scratch += [pltpu.SemaphoreType.DMA((2 * STEPS + 3,))]
     scratch += [pltpu.SemaphoreType.DMA((2, k)) for k in (1, 3 * n, 3 * n, 7 * n, 3 * n, 3 * n, 4 * n)]
     return pl.pallas_call(
         main_kernel,
         in_specs=[hbm] * 5,
-        out_specs=[pl.BlockSpec(memory_space=pltpu.VMEM), hbm],
-        out_shape=[jax.ShapeDtypeStruct((W, W), f32), jax.ShapeDtypeStruct((ROWS, W), f32)],
+        out_specs=[pl.BlockSpec(memory_space=pltpu.VMEM)] * 5,
+        out_shape=[pltpu.VMEM((ROWS, W), f32)] + [pltpu.VMEM((4, ROWS, HALF), bf16)] * 2 + [pltpu.VMEM((W, W), bf16)] * 2,
         scratch_shapes=scratch,
-        compiler_params=pltpu.CompilerParams(collective_id=0, has_side_effects=True, vmem_limit_bytes=60 << 20),
+        compiler_params=pltpu.CompilerParams(collective_id=0, has_side_effects=True, vmem_limit_bytes=48 << 20),
         name="main",
     )(q_final, r_first, r_second, q_grad, r_grad)
 
 
-def finish_kernel(u, q, m2, out):
-    out[...] = u[...] + mm3(halves(q[...]), halves(m2[...]))
-
-
-def finish(u, q_final, m2):
-    rows = ROWS // 6
-    spec = pl.BlockSpec((rows, W), lambda i: (i, 0))
-    small = pl.BlockSpec((W, W), lambda i: (0, 0))
+def finish_kernel(u, slab_h, slab_l, m2_h, m2_l, out_hbm, out, sem):
+    m2 = m2_h[...], m2_l[...]
+    stores = []
+    for step in range(6):
+        at = slice(step * 256, (step + 1) * 256)
+        q = join([(slab_h[i, at], slab_l[i, at]) for i in (0, 3)], 1)
+        out[at] = u[at] + mm3(q, m2)
+        stores.append(pltpu.make_async_copy(out.at[at], out_hbm.at[at], sem.at[step]))
+        stores[-1].start()
+    for store in stores:
+        store.wait()
+
+
+def finish(*operands):
     return pl.pallas_call(
         finish_kernel,
-        grid=(6,),
-        in_specs=[spec, spec, small],
-        out_specs=spec,
+        in_specs=[pl.BlockSpec(memory_space=pltpu.VMEM)] * 5,
+        out_specs=pl.BlockSpec(memory_space=pl.ANY),
         out_shape=jax.ShapeDtypeStruct((ROWS, W), jnp.float32),
-        compiler_params=pltpu.CompilerParams(vmem_limit_bytes=48 << 20),
+        scratch_shapes=[pltpu.VMEM((ROWS, W), jnp.float32), pltpu.SemaphoreType.DMA((6,))],
+        compiler_params=pltpu.CompilerParams(vmem_limit_bytes=12 << 20),
         name="finish",
-    )(u, q_final, m2)
+    )(*operands)
 
 
 def local(q_final, r_first, r_second, q_grad, r_grad):
-    m2, u = main(q_final, r_first, r_second, q_grad, r_grad)
-    return finish(u, q_final, m2)
+    return finish(*main(q_final, r_first, r_second, q_grad, r_grad))
 
 
 def solution(mesh):

time: 60.2 us -> 49.8 us (0.83)
  Pallas kernels: 56.8 us -> 49.5 us
  local copies, waits for them, and re-layouts: 3.11 us -> 0 us
    pallas_call x1, Pallas kernels: 50 us -> 46.1 us  [main(): pl.pallas_call(main_kernel, in_specs=[hbm] * 5, out_specs=[pl.BlockSpec(m...]
    pallas_call x1, Pallas kernels: 6.76 us -> 3.45 us  [finish(): pl.pallas_call(finish_kernel, in_specs=[pl.BlockSpec(memory_space=pltpu.V...]
    unnamed x4 -> x0, local copies, waits for them, and re-layouts: 3.11 us -> none
where the time goes in v1:
time: 49.8 us; the launch traced here: 49.7 us
  Pallas kernels  49.5 us (99%)
    pallas_call x1, Pallas kernels, main(): pl.pallas_call(main_kernel, in_specs=[hbm] * 5, out_specs=[pl.BlockSpec(m...  46.1 us
    pallas_call x1, Pallas kernels, finish(): pl.pallas_call(finish_kernel, in_specs=[pl.BlockSpec(memory_space=pltpu.V...  3.45 us

profile of v1, /device:TPU:1, one launch (start us, length us, event | category | flops | bytes accessed | tf_op | source)
XLA Modules:
  0.0 49.7 jit_solution(6719194259788788385)
XLA Ops:
  0.0 46.1 %main.1 = (f32[1536,512]{1,0:T(8,128)S(1)}, bf16[4,1536,256]{2,1,0:T(8,128)(2,1)S(1)}, bf16[4,1536,256]{2,1,0:T(8,128)(2,1)S(1)}, bf16[512,512]{1,0:T(8,128)(2,1)S(1)}, bf16[512,512]{1,0:T(8,128)(2,1)S(1)}) custom-call(f32[1536,512]{1,0:T(8,128)} %q_hbm.1, f32[512,512]{1,0:T(8,128)} %r1_hbm.1, f32[512,512]{1,0:T(8,128)} %r2_hbm.1, f32[1536,512]{1,0:T(8,128)} %g_hbm.1, ...), custom_call_target="tpu_custom_call" | custom-call | tf_op jit(solution)/shard_map/main/pallas_call | solution.py:341
  46.1 3.4 %finish.1 = f32[1536,512]{1,0:T(8,128)} custom-call(f32[1536,512]{1,0:T(8,128)S(1)} %get-tuple-element.10.u, bf16[4,1536,256]{2,1,0:T(8,128)(2,1)S(1)} %get-tuple-element.11.slab_h, bf16[4,1536,256]{2,1,0:T(8,128)(2,1)S(1)} %get-tuple-element.12.slab_l, bf16[512,512]{1,0:T(8,128)(2,1)S(1)} %get-tuple-element.13.m2_h, bf16[512,512]{1,0:T(8,128)(2,1)S(1)} %get-tuple-element.14.m2_l), custom_call_target="tpu_custom_call" | custom-call | tf_op jit(solution)/shard_map/finish/pallas_call | solution.py:366

commit v2 on v1

--- a/solution.py
+++ b/solution.py
@@ -9,7 +9,8 @@
 W, HALF = 512, 256
 NX, NY, NZ = 4, 4, 8
 ROWS, STEPS = 1536, 3
-PARTS = ((0, 5, True), (5, 4, False))
+PARTS = ((0, 4, True), (4, 4, False))
+SLOTS = ((0, 5), (5, 9))
 FAR_4, FAR_8 = (1, 0, 2), (3, 2, 4, 1, 5, 0, 6)
 NN, NT, TN = ((1,), (0,)), ((1,), (1,)), ((0,), (0,))
 A, B = slice(0, HALF), slice(HALF, W)
@@ -93,14 +94,15 @@
     is_top = jnp.full((HALF, HALF), h, jnp.int32) == 0
     parts = (jnp.where(low & is_top, square, wide[:, A]), jnp.where(low | is_top, wide[:, B], square))
     diag = jnp.sum(jnp.where(eye, jnp.where(is_top, wide[:, A], square), 0.0), axis=0, keepdims=True)
-    first = lax.broadcasted_iota(jnp.int32, (8, 128), 0) == 0
+    first = lax.broadcasted_iota(jnp.int32, (8, 128), 0)
     for group in range(16):
         for tile in range(8):
             r, l = group * 16 + (tile // 4) * 8, (tile % 4) * 128
             put(group // 4, group % 4, tile, parts[l // HALF][r : r + 8, l % HALF : l % HALF + 128])
         extra = jnp.zeros((8, 128), jnp.float32)
-        if group < 2:
-            extra = jnp.where(first, jnp.broadcast_to(diag[:, group * 128 : group * 128 + 128], (8, 128)), 0.0)
+        if group == 0:
+            lines = [jnp.broadcast_to(diag[:, i * 128 : i * 128 + 128], (8, 128)) for i in range(2)]
+            extra = jnp.where(first == 0, lines[0], jnp.where(first == 1, lines[1], 0.0))
         put(group // 4, group % 4, 8, extra)
 
 
@@ -150,7 +152,8 @@
     r2_p, inv1_p, inv2_p, both_p = (tuple(bf[i : i + 2]) for i in range(0, 8, 2))
     theirs, core_in, mine, own, z_in, whole = (scratch.pop(0) for _ in range(6))
     one_in, two, two_in = ([scratch.pop(0) for _ in PARTS] for _ in range(3))
-    in_sem, core_sem, one_sem, two_sem, z_sem, four_sem, five_sem, last_sem = (scratch.pop(0) for _ in range(8))
+    e_in, lines = scratch.pop(0), scratch.pop(0)
+    in_sem, core_sem, one_sem, two_sem, z_sem, four_sem, five_sem, last_sem, e_sem = (scratch.pop(0) for _ in range(9))
     x, y, z, c = place()
     other = device(x, y, z, 1 - c)
     xs = [lax.rem(x + k, NX) for k in range(1, NX)]
@@ -226,6 +229,7 @@
     def line(ref, part, at):
         return ref.at[at, :, span(part)] if part[2] else ref.at[:, at, span(part)]
 
+    e_copies = [send(mine.at[0, 0, 8], e_in.at[k], e_sem, k, to_x[k]) for k in FAR_4]
     one = [[send(line(mine, part, (xs if part[2] else ys)[k]), one_in[p].at[k], one_sem, 3 * p + k, (to_x if part[2] else to_y)[k])
             for k in FAR_4] for p, part in enumerate(PARTS)]
 
@@ -239,7 +243,12 @@
         for copy in one[p]:
             copy.wait_recv()
         here = mine[x, :, lo:hi] if part[2] else mine[:, y, lo:hi]
-        two[p][...] = (here + one_in[p][0]) + (one_in[p][1] + one_in[p][2])
+        two[p][:, 0 : part[1]] = (here + one_in[p][0]) + (one_in[p][1] + one_in[p][2])
+        if p == 0:
+            for copy in e_copies:
+                copy.wait_recv()
+            line_sum = (mine[0, 0, 8] + e_in[0]) + (e_in[1] + e_in[2])
+            two[p][:, 4] = jnp.broadcast_to(line_sum[None], (4, 8, 128))
         two_copies.append([send(two[p].at[(ys if part[2] else xs)[k]], two_in[p].at[k], two_sem, 3 * p + k, (to_y if part[2] else to_x)[k])
                            for k in FAR_4])
 
@@ -251,11 +260,11 @@
 
     z_copies = []
     for p, part in enumerate(PARTS):
-        lo, hi = part[0], part[0] + part[1]
+        lo, hi = SLOTS[p]
         for copy in two_copies[p]:
             copy.wait_recv()
         own[lo:hi] = (two[p][y if part[2] else x] + two_in[p][0]) + (two_in[p][1] + two_in[p][2])
-        z_copies.append([send(own.at[span(part)], z_in.at[k, span(part)], z_sem, 7 * p + k, to_z[k]) for k in FAR_8])
+        z_copies.append([send(own.at[pl.ds(lo, hi - lo)], z_in.at[k, pl.ds(lo, hi - lo)], z_sem, 7 * p + k, to_z[k]) for k in FAR_8])
 
     small = small_inverses((r1[...], r2[...]))
     for m, out in enumerate((inv1, inv2)):
@@ -276,13 +285,15 @@
 
     four = []
     for p, part in enumerate(PARTS):
-        lo, hi = part[0], part[0] + part[1]
+        lo, hi = SLOTS[p]
         for copy in z_copies[p]:
             copy.wait_recv()
         total = own[lo:hi]
         for k in range(NZ - 1):
             total = total + z_in[k, lo:hi]
-        whole[c, x, y, lo:hi] = total
+        whole[c, x, y, part[0] : part[0] + part[1]] = total[0 : part[1]]
+        if p == 0:
+            lines[c] = total[4]
         ref = whole.at[c, x, y, span(part)]
         four.append([send(ref, ref, four_sem, 3 * p + k, (to_y if part[2] else to_x)[k]) for k in FAR_4])
     for step in range(STEPS):
@@ -292,7 +303,7 @@
         u_buf[at, B] = mm3(g1, cut(both, B, B), NT)
 
     five = []
-    last = []
+    last = [send(lines.at[c], lines.at[c], e_sem, 3, other)]
     mine_all = whole.at[c]
     for p, part in enumerate(PARTS):
         for copy in four[p]:
@@ -313,9 +324,8 @@
         for tile in range(8):
             r, l = group * 16 + (tile // 4) * 8, (tile % 4) * 128
             square[r : r + 8, l : l + 128] = whole[(*at, tile)]
-        if group % 16 < 2:
-            l = group // 16 * HALF + group % 16 * 128
-            diag[:, l : l + 128] = whole[(*at, 8)]
+    for i in range(4):
+        diag[0:1, i * 128 : i * 128 + 128] = lines[i // 2, i % 2 : i % 2 + 1]
     for s, m in zip((A, B), middle(square, diag[0:1], k1, k2, pair_of(r2_p), pair_of(inv1_p), pair_of(inv2_p), pair_of(both_p))):
         m2_h[s], m2_l[s] = halves(m)
     for copy in sent:
@@ -333,11 +343,12 @@
     scratch += [pltpu.VMEM((NX, NY, 9, *tile), f32)] * 3
     scratch += [pltpu.VMEM((9, *tile), f32), pltpu.VMEM((NZ - 1, 9, *tile), f32), pltpu.VMEM((2, NX, NY, 9, *tile), f32)]
     scratch += [pltpu.VMEM((3, 4, part[1], *tile), f32) for part in PARTS]
-    scratch += [pltpu.VMEM((4, part[1], *tile), f32) for part in PARTS]
-    scratch += [pltpu.VMEM((3, part[1], *tile), f32) for part in PARTS]
+    scratch += [pltpu.VMEM((4, hi - lo, *tile), f32) for lo, hi in SLOTS]
+    scratch += [pltpu.VMEM((3, hi - lo, *tile), f32) for lo, hi in SLOTS]
+    scratch += [pltpu.VMEM((3, *tile), f32), pltpu.VMEM((2, *tile), f32)]
     n = len(PARTS)
     scratch += [pltpu.SemaphoreType.DMA((2 * STEPS + 3,))]
-    scratch += [pltpu.SemaphoreType.DMA((2, k)) for k in (1, 3 * n, 3 * n, 7 * n, 3 * n, 3 * n, 4 * n)]
+    scratch += [pltpu.SemaphoreType.DMA((2, k)) for k in (1, 3 * n, 3 * n, 7 * n, 3 * n, 3 * n, 4 * n, 4)]
     return pl.pallas_call(
         main_kernel,
         in_specs=[hbm] * 5,

time: 49.8 us -> 49.2 us (0.988)
  Pallas kernels: 49.5 us -> 49 us
    pallas_call x1, Pallas kernels: 46.1 us -> 45.5 us  [main(): pl.pallas_call(main_kernel, in_specs=[hbm] * 5, out_specs=[pl.BlockSpec(m...]
where the time goes in v2:
time: 49.2 us; the launch traced here: 49.1 us
  Pallas kernels  49 us (100%)
    pallas_call x1, Pallas kernels, main(): pl.pallas_call(main_kernel, in_specs=[hbm] * 5, out_specs=[pl.BlockSpec(m...  45.5 us
    pallas_call x1, Pallas kernels, finish(): pl.pallas_call(finish_kernel, in_specs=[pl.BlockSpec(memory_space=pltpu.V...  3.45 us

profile of v2, /device:TPU:1, one launch (start us, length us, event | category | flops | bytes accessed | tf_op | source)
XLA Modules:
  0.0 49.1 jit_solution(14069417908962440948)
XLA Ops:
  0.0 45.5 %main.1 = (f32[1536,512]{1,0:T(8,128)S(1)}, bf16[4,1536,256]{2,1,0:T(8,128)(2,1)S(1)}, bf16[4,1536,256]{2,1,0:T(8,128)(2,1)S(1)}, bf16[512,512]{1,0:T(8,128)(2,1)S(1)}, bf16[512,512]{1,0:T(8,128)(2,1)S(1)}) custom-call(f32[1536,512]{1,0:T(8,128)} %q_hbm.1, f32[512,512]{1,0:T(8,128)} %r1_hbm.1, f32[512,512]{1,0:T(8,128)} %r2_hbm.1, f32[1536,512]{1,0:T(8,128)} %g_hbm.1, ...), custom_call_target="tpu_custom_call" | custom-call | tf_op jit(solution)/shard_map/main/pallas_call | solution.py:352
  45.5 3.4 %finish.1 = f32[1536,512]{1,0:T(8,128)} custom-call(f32[1536,512]{1,0:T(8,128)S(1)} %get-tuple-element.10.u, bf16[4,1536,256]{2,1,0:T(8,128)(2,1)S(1)} %get-tuple-element.11.slab_h, bf16[4,1536,256]{2,1,0:T(8,128)(2,1)S(1)} %get-tuple-element.12.slab_l, bf16[512,512]{1,0:T(8,128)(2,1)S(1)} %get-tuple-element.13.m2_h, bf16[512,512]{1,0:T(8,128)(2,1)S(1)} %get-tuple-element.14.m2_l), custom_call_target="tpu_custom_call" | custom-call | tf_op jit(solution)/shard_map/finish/pallas_call | solution.py:377

commit v3 on v2

--- a/solution.py
+++ b/solution.py
@@ -237,6 +237,12 @@
         load.wait()
     r2_p[0][...], r2_p[1][...] = halves(r2[...])
 
+    r2_v = pair_of(r2_p)
+    r1_v, rg_v = halves(r1[...]), halves(rg[...])
+    t = halves(jnp.concatenate([mm3(cut(r1_v, A), rg_v, NT), mm3(cut(r1_v, B, B), cut(rg_v, slice(None), B), NT)], axis=0))
+    k2[A, A], k2[B] = mm3(cut(r2_v, A), cut(t, slice(None), A)), mm3(cut(r2_v, B, B), cut(t, B))
+    k1[:, A], k1[B, B] = mm3(cut(t, slice(None), A), cut(r2_v, A, A)), mm3(cut(t, B), cut(r2_v, slice(None), B))
+
     two_copies = []
     for p, part in enumerate(PARTS):
         lo, hi = part[0], part[0] + part[1]
@@ -251,12 +257,6 @@
             two[p][:, 4] = jnp.broadcast_to(line_sum[None], (4, 8, 128))
         two_copies.append([send(two[p].at[(ys if part[2] else xs)[k]], two_in[p].at[k], two_sem, 3 * p + k, (to_y if part[2] else to_x)[k])
                            for k in FAR_4])
-
-    r2_v = pair_of(r2_p)
-    r1_v, rg_v = halves(r1[...]), halves(rg[...])
-    t = halves(jnp.concatenate([mm3(cut(r1_v, A), rg_v, NT), mm3(cut(r1_v, B, B), cut(rg_v, slice(None), B), NT)], axis=0))
-    k2[A, A], k2[B] = mm3(cut(r2_v, A), cut(t, slice(None), A)), mm3(cut(r2_v, B, B), cut(t, B))
-    k1[:, A], k1[B, B] = mm3(cut(t, slice(None), A), cut(r2_v, A, A)), mm3(cut(t, B), cut(r2_v, slice(None), B))
 
     z_copies = []
     for p, part in enumerate(PARTS):

time: 49.2 us -> 49.2 us (level)
  no operation moved by 1% of the time
where the time goes in v3:
time: 49.2 us
  Pallas kernels  49 us (100%)
    pallas_call x1, Pallas kernels, main(): pl.pallas_call(main_kernel, in_specs=[hbm] * 5, out_specs=[pl.BlockSpec(m...  45.5 us
    pallas_call x1, Pallas kernels, finish(): pl.pallas_call(finish_kernel, in_specs=[pl.BlockSpec(memory_space=pltpu.V...  3.45 us

profile of v3, /device:TPU:1, one launch (start us, length us, event | category | flops | bytes accessed | tf_op | source)
XLA Modules:
  0.0 49.2 jit_solution(15952512192256128867)
XLA Ops:
  0.0 45.5 %main.1 = (f32[1536,512]{1,0:T(8,128)S(1)}, bf16[4,1536,256]{2,1,0:T(8,128)(2,1)S(1)}, bf16[4,1536,256]{2,1,0:T(8,128)(2,1)S(1)}, bf16[512,512]{1,0:T(8,128)(2,1)S(1)}, bf16[512,512]{1,0:T(8,128)(2,1)S(1)}) custom-call(f32[1536,512]{1,0:T(8,128)} %q_hbm.1, f32[512,512]{1,0:T(8,128)} %r1_hbm.1, f32[512,512]{1,0:T(8,128)} %r2_hbm.1, f32[1536,512]{1,0:T(8,128)} %g_hbm.1, ...), custom_call_target="tpu_custom_call" | custom-call | tf_op jit(solution)/shard_map/main/pallas_call | solution.py:352
  45.5 3.4 %finish.1 = f32[1536,512]{1,0:T(8,128)} custom-call(f32[1536,512]{1,0:T(8,128)S(1)} %get-tuple-element.10.u, bf16[4,1536,256]{2,1,0:T(8,128)(2,1)S(1)} %get-tuple-element.11.slab_h, bf16[4,1536,256]{2,1,0:T(8,128)(2,1)S(1)} %get-tuple-element.12.slab_l, bf16[512,512]{1,0:T(8,128)(2,1)S(1)} %get-tuple-element.13.m2_h, bf16[512,512]{1,0:T(8,128)(2,1)S(1)} %get-tuple-element.14.m2_l), custom_call_target="tpu_custom_call" | custom-call | tf_op jit(solution)/shard_map/finish/pallas_call | solution.py:377
